TPU v7x, 128 devices: a whole 4x4x4 slice. The times are simulated.
128 devices in a mesh: zero: 16 (over y, x), cols: 8 (over z, core).
Axes of the slice: x: 4, y: 4, z: 4, core: 2. Of those that a mesh axis runs over, the one named last changes fastest.
Arguments:
- train_gate: bfloat16 [4096, 11008], P('zero', 'cols'), may hold values from -0.125 to 0.125
- low_gate: bfloat16 [4096, 64], P('zero'), may hold values from -0.09375 to 0.09375
- high_gate: bfloat16 [64, 11008], P(None, 'cols'), may hold values from -0.75 to 0.75
- train_up: bfloat16 [4096, 11008], P('zero', 'cols'), may hold values from -0.125 to 0.125
- low_up: bfloat16 [4096, 64], P('zero'), may hold values from -0.09375 to 0.09375
- high_up: bfloat16 [64, 11008], P(None, 'cols'), may hold values from -0.75 to 0.75
- norm_train: float32 [4096], P(('zero', 'cols')), may hold values from 0.25 to 1.75
- norm_step: float32 [4096], P(('zero', 'cols')), may hold values from -0.3 to 0.3
Outputs:
- ready_gate: bfloat16 [4096, 11008], P(None, 'cols')
- ready_up: bfloat16 [4096, 11008], P(None, 'cols')
- factor_gate: float32 [11008], P('cols')
- factor_up: float32 [11008], P('cols')
- serve_norm: bfloat16 [4096], replicated
All inputs are finite; a program needn't handle non-finite values. Where the computation divides by a largest or mean magnitude, that divisor is 1e-20 or more.
Results may differ from a plain program's by a relative error of at most 0.001.
Values may be sent and summed in bfloat16 or wider, within the bound.
A program may use at most 128 MiB of HBM per device.

v0:
```python
import jax
import jax.numpy as jnp
from jax import lax
from jax.sharding import PartitionSpec as P

D_MODEL = 4096


mix_rate = 1.0


def from_everyone(shard, axis):
    peers = lax.axis_size(axis)
    return lax.all_to_all(
        jnp.broadcast_to(shard[None], (peers, *shard.shape)), axis, 0, 0, tiled=True
    )


def taken_together(shard, axis):
    return from_everyone(shard, axis).sum(axis=0)


def packed_total(arrays, axis):
    flat, at, done = (jnp.concatenate([a.reshape(-1) for a in arrays]), 0, [])
    so_far = taken_together(flat, axis)
    for a in arrays:
        done.append(so_far[at : at + a.size].reshape(a.shape))
        at += a.size
    return tuple(done)


def sent_together(arrays, axis, dim, along):
    ends, at = ([], 0)
    for a in arrays[:-1]:
        at += a.shape[along]
        ends.append(at)
    both = jnp.concatenate(arrays, axis=along)
    return tuple(jnp.split(lax.all_gather(both, axis, axis=dim, tiled=True), ends, axis=along))


def shards(train_gate, low_gate, high_gate, train_up, low_up, high_up, norm_train, norm_step):
    latest_gate = train_gate.astype(jnp.float32) + mix_rate * jnp.dot(
        low_gate, high_gate, preferred_element_type=jnp.float32
    )
    latest_up = train_up.astype(jnp.float32) + mix_rate * jnp.dot(
        low_up, high_up, preferred_element_type=jnp.float32
    )
    total_gate, total_up = packed_total(
        (jnp.sum(jnp.abs(latest_gate), axis=0), jnp.sum(jnp.abs(latest_up), axis=0)), "zero"
    )
    factor_gate = total_gate / D_MODEL
    factor_up = total_up / D_MODEL
    narrow_gate, narrow_up = (
        (latest_gate / factor_gate).astype(jnp.bfloat16),
        (latest_up / factor_up).astype(jnp.bfloat16),
    )
    ready_gate, ready_up = sent_together((narrow_gate, narrow_up), "zero", 0, 1)
    serve_norm = lax.all_gather(
        (norm_train + norm_step).astype(jnp.bfloat16), ("zero", "cols"), axis=0, tiled=True
    )
    return (ready_gate, ready_up, factor_gate, factor_up, serve_norm)


def solution(mesh):
    return jax.shard_map(
        shards,
        mesh=mesh,
        in_specs=(
            P("zero", "cols"),
            P("zero", None),
            P(None, "cols"),
            P("zero", "cols"),
            P("zero", None),
            P(None, "cols"),
            P(("zero", "cols")),
            P(("zero", "cols")),
        ),
        out_specs=(P(None, "cols"), P(None, "cols"), P("cols"), P("cols"), P()),
        check_vma=False,
    )
```

profile of v0, /device:TPU:0, one launch (start us, length us, event | category | flops | bytes accessed | tf_op | source)
XLA Modules:
  0.0 200.0 jit_solution(16699252838358729009)
XLA Ops:
  7.2 0.0 copy-start
  7.2 0.0 copy-start.3
  7.2 0.0 copy-start.2
  7.2 0.0 all-gather.2.cloned.1.call-start
  7.2 0.8 copy-done
  8.1 1.7 abs_reduce_fusion.1
  9.8 0.0 copy-done.3
  9.8 0.5 abs_reduce_fusion
  10.4 0.1 pad_maximum_fusion.1
  10.5 0.1 broadcast_in_dim.2
  10.6 15.2 %all_to_all.6 = f32[16,1,2752]{2,1,0:T(1,128)S(1)} all-to-all(f32[16,1,2752]{2,1,0:T(1,128)S(1)} %broadcast_in_dim.2), channel_id=1, replica_groups=mesh['zero'=16,'cols'=8] {'zero'}, dimensions={0} | all-to-all | bytes 352256 | tf_op jit(solution)/shard_map/all_to_all | solution.py:14
  25.8 0.1 reduce_sum.29
  25.9 0.1 slice_multiply_fusion.1
  26.0 0.4 divide_convert_fusion
  26.4 0.2 copy-done.4
  26.5 0.0 copy-done.5
  26.6 1.2 pad_maximum_fusion
  27.7 0.0 all-gather.2.cloned.1.call-update
  27.8 0.6 copy-done.6
  28.4 0.0 copy-done.7
  28.4 0.2 dynamic-update-slice
  28.7 67.0 %all-reduce = bf16[4096]{0:T(1024)(128)(2,1)} all-reduce(bf16[4096]{0:T(1024)(128)(2,1)S(1)} %dynamic-update-slice), channel_id=1, replica_groups=mesh['zero'=16,'cols'=8] {'zero','cols'}, use_global_device_ids=true, to_apply=%add | all-reduce | flops 4096 | bytes 16384
  95.6 81.2 %all-gather.2.cloned.1.call-done = bf16[4096,2752]{0,1:T(8,128)(2,1)} async-done(((bf16[256,2752]{0,1:T(8,128)(2,1)}), bf16[4096,2752]{0,1:T(8,128)(2,1)}) %all-gather.2.cloned.1.call-update) | async-done | bytes 22544400 | tf_op jit(solution)/shard_map/all_gather | solution.py:38
  176.9 16.3 %fusion = (bf16[4096,1376]{0,1:T(8,128)(2,1)}, bf16[4096,1376]{0,1:T(8,128)(2,1)}) fusion(bf16[4096,2752]{0,1:T(8,128)(2,1)} %all-gather.2.cloned.1.call-done), kind=kLoop, calls=%fused_computation.11 | loop fusion | bytes 45088768 | tf_op jit(solution)/shard_map/split | solution.py:38
  (9 shorter events, 0.0 us)
Async XLA Ops:
  7.2 0.9 copy-start
  7.2 2.6 %copy-start.3 = (bf16[256,64]{0,1:T(8,128)(2,1)S(1)}, bf16[256,64]{0,1:T(8,128)(2,1)}, u32[]{:S(2)}) copy-start(bf16[256,64]{0,1:T(8,128)(2,1)} %param.12) | copy-start | bytes 98308
  7.2 2.6 %copy-start.2 = (bf16[64,1376]{1,0:T(8,128)(2,1)S(1)}, bf16[64,1376]{1,0:T(8,128)(2,1)}, u32[]{:S(2)}) copy-start(bf16[64,1376]{1,0:T(8,128)(2,1)} %param.13) | copy-start | bytes 528388
  7.2 169.7 %all-gather.2.cloned.1.call-start = ((), (), s32[]{:S(2)}) async-start(), calls=%async_computation.1 | async-start | bytes 23953408 | tf_op jit(solution)/shard_map/all_gather | solution.py:38
  8.1 1.7 copy-start.1
  25.9 0.6 copy-start.4
  25.9 0.6 copy-start.5
  27.7 0.7 copy-start.6
  27.7 0.7 copy-start.7
Sparse Core Ops, SparseCore 0:
  27.9 148.9 all-gather.1
where the time goes:
time: 200 us
  blocking collectives  82.2 us (41%)
  waiting for transfers between devices  81.3 us (41%)
  local copies, waits for them, and re-layouts  18.3 us (9%)
  between operations  14.1 us (7%)
  matrix products  2.24 us (1%)
    all_gather x1, waiting for transfers between devices, sent_together(): lax.all_gather(both, axis, axis=dim, tiled=True)  81.2 us
    unnamed x1, blocking collectives  67 us
    split x1, local copies, waits for them, and re-layouts, sent_together(): jnp.split(lax.all_gather(both, axis, axis=dim, tiled=True), ends, axis=al...  16.3 us
    all_to_all x1, blocking collectives, from_everyone(): lax.all_to_all(jnp.broadcast_to(shard[None], (peers, *shard.shape)), axis...  15.2 us
  transfers between devices with their start and end apart: 1, of which 1 were waited for; matrix products, arithmetic and copies ran while one was open for 0% of the time, Pallas kernels for 0%

commit v1 on v0

v1 whole, which is shorter than its diff:
```python
import functools

import jax
import jax.numpy as jnp
from jax import lax
from jax.experimental import pallas as pl
from jax.experimental.pallas import tpu as pltpu
from jax.sharding import PartitionSpec as P

MESH = pl.DeviceIdType.MESH
F32 = jnp.float32
BF16 = jnp.bfloat16
SIDE = 4
DIRS = (1, -1)


def wrap(i, n):
    return lax.rem(i + n, n)


def kernel(
    cols,
    rows_total,
    train_g, train_u, low_g, low_u, high_g, high_u, norm_a, norm_b,
    out_g, out_u, factor, norm,
    gains, own, lows, highs, raw, raw_low, latest, part, inverse, sum_x, sum_y,
    gain_sem, in_sem, raw_s, raw_r, low_s, low_r, far_s, far_r, hop_s, hop_r, end_s, end_r, small_s, small_r,
):
    wide, width = own.shape[1:]
    half = wide // 2
    cut = half // 2 // 16 * 16
    pieces = ((0, cut), (cut, half - cut), (half, cut), (half + cut, half - cut))
    zero, col = lax.axis_index("zero"), lax.axis_index("cols")
    x, y = lax.rem(zero, SIDE), lax.div(zero, SIDE)
    train, low, high, out = (train_g, train_u), (low_g, low_u), (high_g, high_u), (out_g, out_u)

    def place(a, along, across):
        dx, dy = (along, across) if a == 0 else (across, along)
        return wrap(y + dy, SIDE) * SIDE + wrap(x + dx, SIDE)

    def block(a, along, across, start, size):
        first = pl.multiple_of(place(a, along, across) * width, width)
        return out[a].at[pl.ds(start, size), pl.ds(first, width)]

    def send(src, dst, ssem, rsem, to):
        return pltpu.make_async_remote_copy(
            src_ref=src, dst_ref=dst, send_sem=ssem, recv_sem=rsem, device_id=to, device_id_type=MESH
        )

    x_peers = [(y * SIDE + wrap(x + o, SIDE), col) for o in range(1, SIDE)]
    y_peers = [(wrap(y + o, SIDE) * SIDE + x, col) for o in range(1, SIDE)]
    c_peers = [(zero, wrap(col + o, cols)) for o in range(1, cols)]

    barrier = pltpu.get_barrier_semaphore()
    for peer in x_peers + y_peers + c_peers:
        pl.semaphore_signal(barrier, inc=1, device_id=peer, device_id_type=MESH)

    gain_loads = [pltpu.make_async_copy(n, gains.at[i], gain_sem.at[i]) for i, n in enumerate((norm_a, norm_b))]
    for load in gain_loads:
        load.start()
    loads = []
    for a in (0, 1):
        loads.append(pltpu.make_async_copy(train[a], own.at[a], in_sem.at[a, 0]))
        loads.append(pltpu.make_async_copy(low[a], lows.at[a], in_sem.at[a, 1]))
        loads.append(pltpu.make_async_copy(high[a], highs.at[a], in_sem.at[a, 2]))
    for load in loads:
        load.start()

    for load in gain_loads:
        load.wait()
    norm[zero, col] = gains[0] + gains[1]
    pl.semaphore_wait(barrier, len(x_peers) + len(y_peers) + len(c_peers))

    sent = []

    def go(copy):
        copy.start()
        sent.append(copy)
        return copy

    def send_raw(p):
        start, size = pieces[p]
        return [
            go(send(train[a].at[pl.ds(start, size), :], raw.at[a, s, pl.ds(start, size), :],
                    raw_s.at[a, s, p], raw_r.at[a, s, p], (place(a, d, 0), col)))
            for a in (0, 1) for s, d in enumerate(DIRS)
        ]

    raws = send_raw(0)
    raws += [
        go(send(low[a], raw_low.at[a, s], low_s.at[a, s], low_r.at[a, s], (place(a, d, 0), col)))
        for a in (0, 1) for s, d in enumerate(DIRS)
    ]
    norm_c = [
        go(send(norm.at[zero, col], norm.at[zero, col], small_s.at[0, i], small_r.at[0, i], peer))
        for i, peer in enumerate(c_peers)
    ]
    for load in loads:
        load.wait()

    padded = part.shape[1]
    for a in (0, 1):
        if padded > wide:
            part[a, wide:, :] = jnp.zeros((padded - wide, part.shape[2]), F32)
        for h in (0, 1):
            r = slice(h * half, (h + 1) * half)
            fresh = own[a, r, :].astype(F32) + lax.dot_general(
                highs[a, :, r], lows[a], (((0,), (0,)), ((), ())), preferred_element_type=F32
            )
            latest[a, r, :] = fresh
            size = jnp.abs(fresh)
            part[a, r, :] = size[:, : width // 2] + size[:, width // 2 :]
        for k in range(padded // 128):
            s = slice(k * 128, (k + 1) * 128)
            sum_x[x, a : a + 1, s] = jnp.sum(part[a, s, :].T, axis=0, keepdims=True)

    sums_x = [
        go(send(sum_x.at[x], sum_x.at[x], small_s.at[1, i], small_r.at[1, i], peer))
        for i, peer in enumerate(x_peers)
    ]
    raws += send_raw(1)
    for copy in norm_c:
        copy.wait_recv()
    norm_x = [
        go(send(norm.at[zero], norm.at[zero], small_s.at[2, i], small_r.at[2, i], peer))
        for i, peer in enumerate(x_peers)
    ]
    for copy in sums_x:
        copy.wait_recv()
    sum_y[y] = sum_x[0] + sum_x[1] + sum_x[2] + sum_x[3]
    sums_y = [
        go(send(sum_y.at[y], sum_y.at[y], small_s.at[3, i], small_r.at[3, i], peer))
        for i, peer in enumerate(y_peers)
    ]
    raws += send_raw(2)
    raws += send_raw(3)
    for copy in norm_x:
        copy.wait_recv()
    row = pl.ds(y * SIDE, SIDE)
    norm_y = [
        go(send(norm.at[row], norm.at[row], small_s.at[4, i], small_r.at[4, i], peer))
        for i, peer in enumerate(y_peers)
    ]
    for copy in sums_y:
        copy.wait_recv()
    scale = (sum_y[0] + sum_y[1] + sum_y[2] + sum_y[3]) * (1.0 / rows_total)
    factor[...] = scale
    for a in (0, 1):
        for k in range(padded // 128):
            s = slice(k * 128, (k + 1) * 128)
            one = 1.0 / factor[a : a + 1, s]
            inverse[a, s, :] = jnp.broadcast_to(one, (128, 128)).T

    def scaled(a, value, r):
        factor_here = inverse[a, r, :]
        return (value * jnp.concatenate([factor_here, factor_here], axis=1)).astype(BF16)

    def finish(a, along, source, low_ref, h):
        r = slice(h * half, (h + 1) * half)
        if source is None:
            value = latest[a, r, :]
        else:
            value = source[r, :].astype(F32) + lax.dot_general(
                highs[a, :, r], low_ref[...], (((0,), (0,)), ((), ())), preferred_element_type=F32
            )
        first = pl.multiple_of(place(a, along, 0) * width, width)
        out[a][r, pl.ds(first, width)] = scaled(a, value, r)

    hops = {}

    def hop(a, q, along, h):
        for s, d in enumerate(DIRS):
            ref = block(a, along, 0, h * half, half)
            hops[a, s, q, h] = go(
                send(ref, ref, hop_s.at[a, s, q, h], hop_r.at[a, s, q, h], (place(a, 0, d), col))
            )

    for h in (0, 1):
        for a in (0, 1):
            finish(a, 0, None, None, h)
            hop(a, 0, 0, h)

    for copy in raws:
        copy.wait_recv()
    far = {}
    for s, d in enumerate(DIRS):
        for a in (0, 1):
            finish(a, -d, raw.at[a, s], raw_low.at[a, s], s)
            ref = block(a, -d, 0, s * half, half)
            far[a, s] = go(send(ref, ref, far_s.at[a, s], far_r.at[a, s], (place(a, d, 0), col)))
    for s, d in enumerate(DIRS):
        for a in (0, 1):
            finish(a, -d, raw.at[a, s], raw_low.at[a, s], 1 - s)
    for s, d in enumerate(DIRS):
        for h in (0, 1):
            for a in (0, 1):
                hop(a, 1 + s, -d, h)
    for h in (0, 1):
        for a in (0, 1):
            far[a, h].wait_recv()
            hop(a, 3, 2, h)
    ends = []
    for q, along in enumerate((0, -1, 1, 2)):
        for s, d in enumerate(DIRS):
            for a in (0, 1):
                hops[a, s, q, s].wait_recv()
                ref = block(a, along, -d, s * half, half)
                ends.append(go(send(ref, ref, end_s.at[a, s, q], end_r.at[a, s, q], (place(a, 0, d), col))))
    for copy in norm_y:
        copy.wait_recv()
    for q in range(4):
        for s in (0, 1):
            for a in (0, 1):
                hops[a, s, q, 1 - s].wait_recv()
    for copy in sent:
        copy.wait_send()
    for copy in ends:
        copy.wait_recv()


def put(g, u, out_g, out_u, sem):
    step = g.shape[0] // 4
    copies = [
        pltpu.make_async_copy(src.at[pl.ds(i * step, step), :], dst.at[pl.ds(i * step, step), :], sem.at[j, i])
        for i in range(4) for j, (src, dst) in enumerate(((g, out_g), (u, out_u)))
    ]
    for copy in copies:
        copy.start()
    for copy in copies:
        copy.wait()


def shards(devices, cols, train_gate, low_gate, high_gate, train_up, low_up, high_up, norm_train, norm_step):
    width, wide = train_gate.shape
    rank = low_gate.shape[1]
    padded = -(-wide // 128) * 128
    rows_total = width * devices
    gain = norm_train.shape[0]
    hbm = pl.BlockSpec(memory_space=pltpu.HBM)
    vmem = pl.BlockSpec(memory_space=pltpu.VMEM)
    dma = pltpu.SemaphoreType.DMA
    out_g, out_u, factor, norm = pl.pallas_call(
        functools.partial(kernel, cols, rows_total),
        out_shape=(
            pltpu.VMEM((wide, rows_total), BF16),
            pltpu.VMEM((wide, rows_total), BF16),
            jax.ShapeDtypeStruct((2, padded), F32),
            jax.ShapeDtypeStruct((devices, cols, 1, gain), F32),
        ),
        in_specs=[hbm] * 8,
        out_specs=[vmem] * 4,
        scratch_shapes=[
            pltpu.VMEM((2, 1, gain), F32),
            pltpu.VMEM((2, wide, width), BF16),
            pltpu.VMEM((2, rank, width), BF16),
            pltpu.VMEM((2, rank, wide), BF16),
            pltpu.VMEM((2, 2, wide, width), BF16),
            pltpu.VMEM((2, 2, rank, width), BF16),
            pltpu.VMEM((2, wide, width), F32),
            pltpu.VMEM((2, padded, width // 2), F32),
            pltpu.VMEM((2, padded, 128), F32),
            pltpu.VMEM((SIDE, 2, padded), F32),
            pltpu.VMEM((SIDE, 2, padded), F32),
            dma((2,)), dma((2, 3)),
            dma((2, 2, 4)), dma((2, 2, 4)),
            dma((2, 2)), dma((2, 2)),
            dma((2, 2)), dma((2, 2)),
            dma((2, 2, 4, 2)), dma((2, 2, 4, 2)),
            dma((2, 2, 4)), dma((2, 2, 4)),
            dma((5, 8)), dma((5, 8)),
        ],
        compiler_params=pltpu.CompilerParams(
            collective_id=0, has_side_effects=True, vmem_limit_bytes=24 * 1024 * 1024
        ),
    )(
        *(
            pltpu.with_memory_space_constraint(array, pltpu.HBM)
            for array in (
                train_gate.T, train_up.T, low_gate.T, low_up.T, high_gate, high_up,
                norm_train.reshape(1, -1), norm_step.reshape(1, -1),
            )
        )
    )
    out_g, out_u = pl.pallas_call(
        put,
        out_shape=(jax.ShapeDtypeStruct((wide, rows_total), BF16),) * 2,
        in_specs=[vmem] * 2,
        out_specs=[hbm] * 2,
        scratch_shapes=[dma((2, 4))],
        compiler_params=pltpu.CompilerParams(vmem_limit_bytes=1024 * 1024),
    )(out_g, out_u)
    return out_g.T, out_u.T, factor[0, :wide], factor[1, :wide], norm.reshape(-1).astype(BF16)


def solution(mesh):
    return jax.shard_map(
        functools.partial(shards, mesh.shape["zero"], mesh.shape["cols"]),
        mesh=mesh,
        in_specs=(
            P("zero", "cols"),
            P("zero", None),
            P(None, "cols"),
            P("zero", "cols"),
            P("zero", None),
            P(None, "cols"),
            P(("zero", "cols")),
            P(("zero", "cols")),
        ),
        out_specs=(P(None, "cols"), P(None, "cols"), P("cols"), P("cols"), P()),
        check_vma=False,
    )
```

time: 200 us -> 136 us (0.68)
  Pallas kernels: 0 us -> 133 us
  blocking collectives: 82.2 us -> 0 us
  waiting for transfers between devices: 81.3 us -> 0 us
  local copies, waits for them, and re-layouts: 18.3 us -> 1.32 us
  between operations: 14.1 us -> 0.65 us
  matrix products: 2.24 us -> 0 us
    pallas_call x0 -> x2, Pallas kernels: none -> 133 us  [the longest x1 126 us: shards(): pl.pallas_call(functools.partial(kernel, cols, rows_total), out_shape=(pl...]
    all_gather x1 -> x0, waiting for transfers between devices: 81.2 us -> none  [sent_together(): lax.all_gather(both, axis, axis=dim, tiled=True)]
    unnamed x1 -> x0, blocking collectives: 67 us -> none
    split x1 -> x0, local copies, waits for them, and re-layouts: 16.3 us -> none  [sent_together(): jnp.split(lax.all_gather(both, axis, axis=dim, tiled=True), ends, axis=al...]
    all_to_all x1 -> x0, blocking collectives: 15.2 us -> none  [from_everyone(): lax.all_to_all(jnp.broadcast_to(shard[None], (peers, *shard.shape)), axis...]
    dot_general x2 -> x0, matrix products: 2.24 us -> none  [the longest x1 1.71 us: shards(): jnp.dot(low_gate, high_gate, preferred_element_type=jnp.float32)]
  transfers between devices with their start and end apart: 1 -> 0, of which waited for: 1 -> 0; matrix products, arithmetic and copies ran while one was open for 0% -> 0% of each run, Pallas kernels for 0% -> 0%
where the time goes in v1:
time: 136 us
  Pallas kernels  133 us (98%)
    pallas_call x1, Pallas kernels, shards(): pl.pallas_call(functools.partial(kernel, cols, rows_total), out_shape=(pl...  126 us
    pallas_call x1, Pallas kernels, shards(): pl.pallas_call(put, out_shape=(jax.ShapeDtypeStruct((wide, rows_total), B...  7.72 us

profile of v1, /device:TPU:0, one launch (start us, length us, event | category | flops | bytes accessed | tf_op | source)
XLA Modules:
  0.0 135.6 jit_solution(11958484427039312945)
XLA Ops:
  0.6 125.7 %shard_map.119 = (bf16[1376,4096]{1,0:T(8,128)(2,1)S(1)}, bf16[1376,4096]{1,0:T(8,128)(2,1)S(1)}, f32[2,1408]{1,0:T(2,128)S(1)}, f32[16,8,1,32]{3,2,1,0:T(1,128)S(1)}) custom-call(bf16[1376,256]{1,0:T(8,128)(2,1)} %bitcast.8, bf16[1376,256]{1,0:T(8,128)(2,1)} %bitcast.9, bf16[64,256]{1,0:T(8,128)(2,1)} %bitcast.10, bf16[64,256]{1,0:T(8,128)(2,1)} %bitcast.11, ...), custom_call_target="tpu_custom_call" | custom-call | tf_op jit(solution)/shard_map/pallas_call | solution.py:242
  126.4 7.7 %shard_map.120 = (bf16[1376,4096]{1,0:T(8,128)(2,1)}, bf16[1376,4096]{1,0:T(8,128)(2,1)}) custom-call(bf16[1376,4096]{1,0:T(8,128)(2,1)S(1)} %get-tuple-element.11.g, bf16[1376,4096]{1,0:T(8,128)(2,1)S(1)} %get-tuple-element.12.u), custom_call_target="tpu_custom_call" | custom-call | tf_op jit(solution)/shard_map/pallas_call | solution.py:284
  134.1 0.6 slice_reduce_fusion
  134.7 0.2 convert_reduce_fusion
  134.9 0.7 convert_element_type.7

commit v2 on v1

--- a/solution.py
+++ b/solution.py
@@ -19,11 +19,10 @@
 
 
 def kernel(
-    cols,
     rows_total,
     train_g, train_u, low_g, low_u, high_g, high_u, norm_a, norm_b,
-    out_g, out_u, factor, norm,
-    gains, own, lows, highs, raw, raw_low, latest, part, inverse, sum_x, sum_y,
+    out_g, out_u, factor, gathered,
+    norm, gains, own, lows, highs, raw, raw_low, latest, part, inverse, sum_x, sum_y,
     gain_sem, in_sem, raw_s, raw_r, low_s, low_r, far_s, far_r, hop_s, hop_r, end_s, end_r, small_s, small_r,
 ):
     wide, width = own.shape[1:]
@@ -49,7 +48,7 @@
 
     x_peers = [(y * SIDE + wrap(x + o, SIDE), col) for o in range(1, SIDE)]
     y_peers = [(wrap(y + o, SIDE) * SIDE + x, col) for o in range(1, SIDE)]
-    c_peers = [(zero, wrap(col + o, cols)) for o in range(1, cols)]
+    c_peers = [(zero, col + 1 - 2 * lax.rem(col, 2))]
 
     barrier = pltpu.get_barrier_semaphore()
     for peer in x_peers + y_peers + c_peers:
@@ -68,7 +67,12 @@
 
     for load in gain_loads:
         load.wait()
-    norm[zero, col] = gains[0] + gains[1]
+    core = lax.rem(col, 2)
+    value = gains[0] + gains[1]
+    spread = jnp.concatenate([value] * (128 // value.shape[1]), axis=1)
+    group = lax.broadcasted_iota(jnp.int32, (1, 128), 1) // value.shape[1]
+    mine = lax.rem(col, 128 // value.shape[1])
+    norm[core, zero] = jnp.where(group == mine, spread, jnp.zeros_like(spread))
     pl.semaphore_wait(barrier, len(x_peers) + len(y_peers) + len(c_peers))
 
     sent = []
@@ -92,7 +96,7 @@
         for a in (0, 1) for s, d in enumerate(DIRS)
     ]
     norm_c = [
-        go(send(norm.at[zero, col], norm.at[zero, col], small_s.at[0, i], small_r.at[0, i], peer))
+        go(send(norm.at[core, zero], norm.at[core, zero], small_s.at[0, i], small_r.at[0, i], peer))
         for i, peer in enumerate(c_peers)
     ]
     for load in loads:
@@ -122,7 +126,7 @@
     for copy in norm_c:
         copy.wait_recv()
     norm_x = [
-        go(send(norm.at[zero], norm.at[zero], small_s.at[2, i], small_r.at[2, i], peer))
+        go(send(norm.at[:, zero], norm.at[:, zero], small_s.at[2, i], small_r.at[2, i], peer))
         for i, peer in enumerate(x_peers)
     ]
     for copy in sums_x:
@@ -138,7 +142,7 @@
         copy.wait_recv()
     row = pl.ds(y * SIDE, SIDE)
     norm_y = [
-        go(send(norm.at[row], norm.at[row], small_s.at[4, i], small_r.at[4, i], peer))
+        go(send(norm.at[:, row], norm.at[:, row], small_s.at[4, i], small_r.at[4, i], peer))
         for i, peer in enumerate(y_peers)
     ]
     for copy in sums_y:
@@ -208,6 +212,8 @@
                 ends.append(go(send(ref, ref, end_s.at[a, s, q], end_r.at[a, s, q], (place(a, 0, d), col))))
     for copy in norm_y:
         copy.wait_recv()
+    for i in range(gathered.shape[0]):
+        gathered[i : i + 1, :] = norm[0, i] + norm[1, i]
     for q in range(4):
         for s in (0, 1):
             for a in (0, 1):
@@ -218,14 +224,39 @@
         copy.wait_recv()
 
 
-def put(g, u, out_g, out_u, sem):
-    step = g.shape[0] // 4
+def copy_out(src, dst, sem):
+    step = src.shape[0] // 4
     copies = [
-        pltpu.make_async_copy(src.at[pl.ds(i * step, step), :], dst.at[pl.ds(i * step, step), :], sem.at[j, i])
-        for i in range(4) for j, (src, dst) in enumerate(((g, out_g), (u, out_u)))
+        pltpu.make_async_copy(src.at[pl.ds(i * step, step), :], dst.at[pl.ds(i * step, step), :], sem.at[i])
+        for i in range(4)
     ]
     for copy in copies:
         copy.start()
+    return copies
+
+
+def put_gate(src, factor, dst, factor_g, factor_u, sem):
+    copies = copy_out(src, dst, sem)
+    wide = factor_g.shape[0]
+    factor_g[...] = factor[0, :wide]
+    factor_u[...] = factor[1, :wide]
+    for copy in copies:
+        copy.wait()
+
+
+def put_up(layers, *refs):
+    src, gains, (dst, norm, rows, sem) = refs[0], refs[1:-4], refs[-4:]
+    copies = copy_out(src, dst, sem)
+    layer = lax.div(lax.axis_index("cols"), 2)
+    parts = norm.shape[0] // gains[0].shape[0]
+    for hi in range(parts):
+        total = jnp.zeros(gains[0].shape, F32)
+        for k, gain in enumerate(gains):
+            source = wrap(layer - k, layers)
+            total = total + jnp.where(source // (layers // parts) == hi, gain[...], jnp.zeros_like(total))
+        for i in range(total.shape[0]):
+            rows[parts * i + hi : parts * i + hi + 1, :] = total[i : i + 1, :]
+    norm[...] = rows[...].astype(BF16)
     for copy in copies:
         copy.wait()
 
@@ -239,17 +270,18 @@
     hbm = pl.BlockSpec(memory_space=pltpu.HBM)
     vmem = pl.BlockSpec(memory_space=pltpu.VMEM)
     dma = pltpu.SemaphoreType.DMA
-    out_g, out_u, factor, norm = pl.pallas_call(
-        functools.partial(kernel, cols, rows_total),
+    out_g, out_u, factor, gathered = pl.pallas_call(
+        functools.partial(kernel, rows_total),
         out_shape=(
             pltpu.VMEM((wide, rows_total), BF16),
             pltpu.VMEM((wide, rows_total), BF16),
             jax.ShapeDtypeStruct((2, padded), F32),
-            jax.ShapeDtypeStruct((devices, cols, 1, gain), F32),
+            jax.ShapeDtypeStruct((devices, 128), F32),
         ),
         in_specs=[hbm] * 8,
         out_specs=[vmem] * 4,
         scratch_shapes=[
+            pltpu.VMEM((2, devices, 1, 128), F32),
             pltpu.VMEM((2, 1, gain), F32),
             pltpu.VMEM((2, wide, width), BF16),
             pltpu.VMEM((2, rank, width), BF16),
@@ -281,15 +313,33 @@
             )
         )
     )
-    out_g, out_u = pl.pallas_call(
-        put,
-        out_shape=(jax.ShapeDtypeStruct((wide, rows_total), BF16),) * 2,
+    layers = cols // 2
+    gains = [gathered] + [
+        lax.ppermute(gathered, "cols", [(i, (i + 2 * k) % cols) for i in range(cols)]) for k in range(1, layers)
+    ]
+    one = jax.ShapeDtypeStruct((wide, rows_total), BF16)
+    small = pltpu.CompilerParams(vmem_limit_bytes=1024 * 1024)
+    cost = pl.CostEstimate(flops=16 * wide * rows_total, bytes_accessed=4 * wide * rows_total, transcendentals=0)
+    out_g, factor_g, factor_u = pl.pallas_call(
+        put_gate,
+        out_shape=(one, jax.ShapeDtypeStruct((wide,), F32), jax.ShapeDtypeStruct((wide,), F32)),
         in_specs=[vmem] * 2,
-        out_specs=[hbm] * 2,
-        scratch_shapes=[dma((2, 4))],
-        compiler_params=pltpu.CompilerParams(vmem_limit_bytes=1024 * 1024),
-    )(out_g, out_u)
-    return out_g.T, out_u.T, factor[0, :wide], factor[1, :wide], norm.reshape(-1).astype(BF16)
+        out_specs=[hbm, vmem, vmem],
+        scratch_shapes=[dma((4,))],
+        compiler_params=small,
+        cost_estimate=cost,
+    )(out_g, factor)
+    rows = devices * cols * gain // 128
+    out_u, norm = pl.pallas_call(
+        functools.partial(put_up, layers),
+        out_shape=(one, jax.ShapeDtypeStruct((rows, 128), BF16)),
+        in_specs=[vmem] * (1 + layers),
+        out_specs=[hbm, vmem],
+        scratch_shapes=[pltpu.VMEM((rows, 128), F32), dma((4,))],
+        compiler_params=small,
+        cost_estimate=cost,
+    )(out_u, *gains)
+    return out_g.T, out_u.T, factor_g, factor_u, norm.reshape(-1)
 
 
 def solution(mesh):

time: 136 us -> 141 us (1.037)
  starting transfers between devices: 0 us -> 6.58 us
    ppermute x0 -> x3, starting transfers between devices: none -> 6.58 us  [shards(): lax.ppermute(gathered, 'cols', [(i, (i + 2 * k) % cols) for i in range(co...]
    pallas_call x2 -> x3, Pallas kernels: 133 us -> 133 us  [the longest x1 124 us: shards(): pl.pallas_call(functools.partial(kernel, rows_total), out_shape=(pltpu.VM...]
  transfers between devices with their start and end apart: 0 -> 3, of which waited for: 0 -> 0; matrix products, arithmetic and copies ran while one was open for 0% -> 0% of each run, Pallas kernels for 0% -> 3%
where the time goes in v2:
time: 141 us
  Pallas kernels  133 us (94%)
  starting transfers between devices  6.58 us (5%)
    pallas_call x1, Pallas kernels, shards(): pl.pallas_call(functools.partial(kernel, rows_total), out_shape=(pltpu.VM...  124 us
    ppermute x3, starting transfers between devices, shards(): lax.ppermute(gathered, 'cols', [(i, (i + 2 * k) % cols) for i in range(co...  6.58 us
    pallas_call x1, Pallas kernels, shards(): pl.pallas_call(functools.partial(put_up, layers), out_shape=(one, jax.Sha...  4.89 us
    pallas_call x1, Pallas kernels, shards(): pl.pallas_call(put_gate, out_shape=(one, jax.ShapeDtypeStruct((wide,), F3...  4.89 us
  transfers between devices with their start and end apart: 3, of which 0 were waited for; matrix products, arithmetic and copies ran while one was open for 0% of the time, Pallas kernels for 3%

profile of v2, /device:TPU:0, one launch (start us, length us, event | category | flops | bytes accessed | tf_op | source)
XLA Modules:
  0.0 140.6 jit_solution(454622172366907486)
XLA Ops:
  0.6 123.5 %shard_map.119 = (bf16[1376,4096]{1,0:T(8,128)(2,1)S(1)}, bf16[1376,4096]{1,0:T(8,128)(2,1)S(1)}, f32[2,1408]{1,0:T(2,128)S(1)}, f32[16,128]{1,0:T(8,128)S(1)}) custom-call(bf16[1376,256]{1,0:T(8,128)(2,1)} %bitcast.9, bf16[1376,256]{1,0:T(8,128)(2,1)} %bitcast.10, bf16[64,256]{1,0:T(8,128)(2,1)} %bitcast.11, bf16[64,256]{1,0:T(8,128)(2,1)} %bitcast.12, ...), custom_call_target="tpu_custom_call" | custom-call | tf_op jit(solution)/shard_map/pallas_call | solution.py:273
  124.2 2.0 %collective-permute-start = (f32[16,128]{1,0:T(8,128)S(1)}, f32[16,128]{1,0:T(8,128)S(1)}, u32[]{:S(2)}, u32[]{:S(2)}) collective-permute-start(f32[16,128]{1,0:T(8,128)S(1)} %get-tuple-element.18.refs_1_), channel_id=1, source_target_pairs={{0,2},{1,3},{2,4},{3,5},{4,6},{5,7},{6,0},{7,1},{8,10},{9,11},{10,... | collective-permute-start | bytes 24584 | tf_op jit(solution)/shard_map/ppermute | solution.py:318
  126.2 3.6 %collective-permute-start.1 = (f32[16,128]{1,0:T(8,128)S(1)}, f32[16,128]{1,0:T(8,128)S(1)}, u32[]{:S(2)}, u32[]{:S(2)}) collective-permute-start(f32[16,128]{1,0:T(8,128)S(1)} %get-tuple-element.18.refs_1_), channel_id=1, source_target_pairs={{0,4},{1,5},{2,6},{3,7},{4,0},{5,1},{6,2},{7,3},{8,12},{9,13},{10,... | collective-permute-start | bytes 24584 | tf_op jit(solution)/shard_map/ppermute | solution.py:318
  129.8 1.0 collective-permute-start.2
  130.8 4.9 %shard_map.120 = (bf16[1376,4096]{1,0:T(8,128)(2,1)}, f32[1376]{0:T(1024)}, f32[1376]{0:T(1024)}) custom-call(bf16[1376,4096]{1,0:T(8,128)(2,1)S(1)} %get-tuple-element.14.src, f32[2,1408]{1,0:T(2,128)S(1)} %get-tuple-element.15.factor), custom_call_target="tpu_custom_call" | custom-call | flops 90177536 | bytes 22544384 | tf_op jit(solution)/shard_map/pallas_call | solution.py:323
  135.7 0.0 collective-permute-done.refs_2_
  135.7 0.0 collective-permute-done.1.refs_3_
  135.7 0.0 collective-permute-done.2.refs_4_
  135.7 4.9 %shard_map.121 = (bf16[1376,4096]{1,0:T(8,128)(2,1)}, bf16[32,128]{1,0:T(8,128)(2,1)}) custom-call(bf16[1376,4096]{1,0:T(8,128)(2,1)S(1)} %get-tuple-element.17.refs_0_, f32[16,128]{1,0:T(8,128)S(1)} %get-tuple-element.18.refs_1_, f32[16,128]{1,0:T(8,128)S(1)} %collective-permute-done.refs_2_, f32[16,128]{1,0:T(8,128)S(1)} %collective-permute-done.1.refs_3_, ...), custom_call_target="tpu_custom_call" | custom-call | flops 90177536 | bytes 22544384 | tf_op jit(solution)/shard_map/pallas_call | solution.py:333
Async XLA Ops:
  124.2 11.5 %collective-permute-start = (f32[16,128]{1,0:T(8,128)S(1)}, f32[16,128]{1,0:T(8,128)S(1)}, u32[]{:S(2)}, u32[]{:S(2)}) collective-permute-start(f32[16,128]{1,0:T(8,128)S(1)} %get-tuple-element.18.refs_1_), channel_id=1, source_target_pairs={{0,2},{1,3},{2,4},{3,5},{4,6},{5,7},{6,0},{7,1},{8,10},{9,11},{10,... | collective-permute-start | bytes 24584 | tf_op jit(solution)/shard_map/ppermute | solution.py:318
  126.2 9.5 %collective-permute-start.1 = (f32[16,128]{1,0:T(8,128)S(1)}, f32[16,128]{1,0:T(8,128)S(1)}, u32[]{:S(2)}, u32[]{:S(2)}) collective-permute-start(f32[16,128]{1,0:T(8,128)S(1)} %get-tuple-element.18.refs_1_), channel_id=1, source_target_pairs={{0,4},{1,5},{2,6},{3,7},{4,0},{5,1},{6,2},{7,3},{8,12},{9,13},{10,... | collective-permute-start | bytes 24584 | tf_op jit(solution)/shard_map/ppermute | solution.py:318
  129.8 5.9 %collective-permute-start.2 = (f32[16,128]{1,0:T(8,128)S(1)}, f32[16,128]{1,0:T(8,128)S(1)}, u32[]{:S(2)}, u32[]{:S(2)}) collective-permute-start(f32[16,128]{1,0:T(8,128)S(1)} %get-tuple-element.18.refs_1_), channel_id=1, source_target_pairs={{0,6},{1,7},{2,0},{3,1},{4,2},{5,3},{6,4},{7,5},{8,14},{9,15},{10,... | collective-permute-start | bytes 24584 | tf_op jit(solution)/shard_map/ppermute | solution.py:318

commit v3 on v1

--- a/solution.py
+++ b/solution.py
@@ -19,12 +19,12 @@
 
 
 def kernel(
-    cols,
+    layers,
     rows_total,
     train_g, train_u, low_g, low_u, high_g, high_u, norm_a, norm_b,
-    out_g, out_u, factor, norm,
-    gains, own, lows, highs, raw, raw_low, latest, part, inverse, sum_x, sum_y,
-    gain_sem, in_sem, raw_s, raw_r, low_s, low_r, far_s, far_r, hop_s, hop_r, end_s, end_r, small_s, small_r,
+    out_g, out_u, factor, norm_out,
+    norm, stack, rows, gains, own, lows, highs, raw, raw_low, latest, part, inverse, sum_x, sum_y,
+    gain_sem, in_sem, raw_s, raw_r, low_s, low_r, far_s, far_r, hop_s, hop_r, end_s, end_r, small_s, small_r, layer_s, layer_r,
 ):
     wide, width = own.shape[1:]
     half = wide // 2
@@ -49,7 +49,7 @@
 
     x_peers = [(y * SIDE + wrap(x + o, SIDE), col) for o in range(1, SIDE)]
     y_peers = [(wrap(y + o, SIDE) * SIDE + x, col) for o in range(1, SIDE)]
-    c_peers = [(zero, wrap(col + o, cols)) for o in range(1, cols)]
+    c_peers = [(zero, col + 1 - 2 * lax.rem(col, 2))]
 
     barrier = pltpu.get_barrier_semaphore()
     for peer in x_peers + y_peers + c_peers:
@@ -58,6 +58,12 @@
     gain_loads = [pltpu.make_async_copy(n, gains.at[i], gain_sem.at[i]) for i, n in enumerate((norm_a, norm_b))]
     for load in gain_loads:
         load.start()
+    core, layer = lax.rem(col, 2), lax.div(col, 2)
+    for other in range(1, layers):
+        @pl.when(other > layer)
+        def _():
+            pl.semaphore_signal(barrier, inc=1, device_id=(zero, 2 * other + core), device_id_type=MESH)
+
     loads = []
     for a in (0, 1):
         loads.append(pltpu.make_async_copy(train[a], own.at[a], in_sem.at[a, 0]))
@@ -68,8 +74,12 @@
 
     for load in gain_loads:
         load.wait()
-    norm[zero, col] = gains[0] + gains[1]
-    pl.semaphore_wait(barrier, len(x_peers) + len(y_peers) + len(c_peers))
+    value = gains[0] + gains[1]
+    spread = jnp.concatenate([value] * (128 // value.shape[1]), axis=1)
+    group = lax.broadcasted_iota(jnp.int32, (1, 128), 1) // value.shape[1]
+    mine = lax.rem(col, 128 // value.shape[1])
+    norm[core, zero] = jnp.where(group == mine, spread, jnp.zeros_like(spread))
+    pl.semaphore_wait(barrier, len(x_peers) + len(y_peers) + len(c_peers) + layer)
 
     sent = []
 
@@ -92,7 +102,7 @@
         for a in (0, 1) for s, d in enumerate(DIRS)
     ]
     norm_c = [
-        go(send(norm.at[zero, col], norm.at[zero, col], small_s.at[0, i], small_r.at[0, i], peer))
+        go(send(norm.at[core, zero], norm.at[core, zero], small_s.at[0, i], small_r.at[0, i], peer))
         for i, peer in enumerate(c_peers)
     ]
     for load in loads:
@@ -122,7 +132,7 @@
     for copy in norm_c:
         copy.wait_recv()
     norm_x = [
-        go(send(norm.at[zero], norm.at[zero], small_s.at[2, i], small_r.at[2, i], peer))
+        go(send(norm.at[:, zero], norm.at[:, zero], small_s.at[2, i], small_r.at[2, i], peer))
         for i, peer in enumerate(x_peers)
     ]
     for copy in sums_x:
@@ -138,7 +148,7 @@
         copy.wait_recv()
     row = pl.ds(y * SIDE, SIDE)
     norm_y = [
-        go(send(norm.at[row], norm.at[row], small_s.at[4, i], small_r.at[4, i], peer))
+        go(send(norm.at[:, row], norm.at[:, row], small_s.at[4, i], small_r.at[4, i], peer))
         for i, peer in enumerate(y_peers)
     ]
     for copy in sums_y:
@@ -199,6 +209,21 @@
         for a in (0, 1):
             far[a, h].wait_recv()
             hop(a, 3, 2, h)
+    for copy in norm_y:
+        copy.wait_recv()
+    for i in range(stack.shape[1]):
+        stack[layer, i : i + 1, :] = norm[0, i] + norm[1, i]
+
+    def to_layer(other):
+        return send(stack.at[layer], stack.at[layer], layer_s.at[other], layer_r.at[layer], (zero, 2 * other + core))
+
+    def from_layer(other):
+        return send(stack.at[other], stack.at[other], layer_s.at[other], layer_r.at[other], (zero, 2 * other + core))
+
+    for other in range(layers):
+        @pl.when(other < layer)
+        def _():
+            to_layer(other).start()
     ends = []
     for q, along in enumerate((0, -1, 1, 2)):
         for s, d in enumerate(DIRS):
@@ -206,8 +231,27 @@
                 hops[a, s, q, s].wait_recv()
                 ref = block(a, along, -d, s * half, half)
                 ends.append(go(send(ref, ref, end_s.at[a, s, q], end_r.at[a, s, q], (place(a, 0, d), col))))
-    for copy in norm_y:
-        copy.wait_recv()
+        if q == 1:
+            for other in range(layers):
+                @pl.when(other > layer)
+                def _():
+                    from_layer(other).wait_recv()
+                    to_layer(other).start()
+    for other in range(layers):
+        @pl.when(other < layer)
+        def _():
+            from_layer(other).wait_recv()
+
+        @pl.when(other != layer)
+        def _():
+            to_layer(other).wait_send()
+    parts = rows.shape[0] // stack.shape[1]
+    for hi in range(parts):
+        here = range(hi * layers // parts, (hi + 1) * layers // parts)
+        total = sum(stack[k] for k in here)
+        for i in range(total.shape[0]):
+            rows[parts * i + hi : parts * i + hi + 1, :] = total[i : i + 1, :]
+    norm_out[...] = rows[...].astype(BF16)
     for q in range(4):
         for s in (0, 1):
             for a in (0, 1):
@@ -218,14 +262,19 @@
         copy.wait_recv()
 
 
-def put(g, u, out_g, out_u, sem):
-    step = g.shape[0] // 4
+def put(g, u, factor, norm, out_g, out_u, factor_g, factor_u, norm_out, sem):
+    pieces = sem.shape[1]
+    step = g.shape[0] // pieces
     copies = [
         pltpu.make_async_copy(src.at[pl.ds(i * step, step), :], dst.at[pl.ds(i * step, step), :], sem.at[j, i])
-        for i in range(4) for j, (src, dst) in enumerate(((g, out_g), (u, out_u)))
+        for i in range(pieces) for j, (src, dst) in enumerate(((g, out_g), (u, out_u)))
     ]
     for copy in copies:
         copy.start()
+    wide = factor_g.shape[0]
+    factor_g[...] = factor[0, :wide]
+    factor_u[...] = factor[1, :wide]
+    norm_out[...] = norm[...]
     for copy in copies:
         copy.wait()
 
@@ -236,20 +285,25 @@
     padded = -(-wide // 128) * 128
     rows_total = width * devices
     gain = norm_train.shape[0]
+    layers = cols // 2
+    rows = devices * cols * gain // 128
     hbm = pl.BlockSpec(memory_space=pltpu.HBM)
     vmem = pl.BlockSpec(memory_space=pltpu.VMEM)
     dma = pltpu.SemaphoreType.DMA
     out_g, out_u, factor, norm = pl.pallas_call(
-        functools.partial(kernel, cols, rows_total),
+        functools.partial(kernel, layers, rows_total),
         out_shape=(
             pltpu.VMEM((wide, rows_total), BF16),
             pltpu.VMEM((wide, rows_total), BF16),
             jax.ShapeDtypeStruct((2, padded), F32),
-            jax.ShapeDtypeStruct((devices, cols, 1, gain), F32),
+            jax.ShapeDtypeStruct((rows, 128), BF16),
         ),
         in_specs=[hbm] * 8,
         out_specs=[vmem] * 4,
         scratch_shapes=[
+            pltpu.VMEM((2, devices, 1, 128), F32),
+            pltpu.VMEM((layers, devices, 128), F32),
+            pltpu.VMEM((rows, 128), F32),
             pltpu.VMEM((2, 1, gain), F32),
             pltpu.VMEM((2, wide, width), BF16),
             pltpu.VMEM((2, rank, width), BF16),
@@ -267,7 +321,8 @@
             dma((2, 2)), dma((2, 2)),
             dma((2, 2, 4, 2)), dma((2, 2, 4, 2)),
             dma((2, 2, 4)), dma((2, 2, 4)),
-            dma((5, 8)), dma((5, 8)),
+            dma((5, 3)), dma((5, 3)),
+            dma((layers,)), dma((layers,)),
         ],
         compiler_params=pltpu.CompilerParams(
             collective_id=0, has_side_effects=True, vmem_limit_bytes=24 * 1024 * 1024
@@ -281,15 +336,21 @@
             )
         )
     )
-    out_g, out_u = pl.pallas_call(
+    out_g, out_u, factor_g, factor_u, norm = pl.pallas_call(
         put,
-        out_shape=(jax.ShapeDtypeStruct((wide, rows_total), BF16),) * 2,
-        in_specs=[vmem] * 2,
-        out_specs=[hbm] * 2,
+        out_shape=(
+            jax.ShapeDtypeStruct((wide, rows_total), BF16),
+            jax.ShapeDtypeStruct((wide, rows_total), BF16),
+            jax.ShapeDtypeStruct((wide,), F32),
+            jax.ShapeDtypeStruct((wide,), F32),
+            jax.ShapeDtypeStruct((rows, 128), BF16),
+        ),
+        in_specs=[vmem] * 4,
+        out_specs=[hbm] * 2 + [vmem] * 3,
         scratch_shapes=[dma((2, 4))],
         compiler_params=pltpu.CompilerParams(vmem_limit_bytes=1024 * 1024),
-    )(out_g, out_u)
-    return out_g.T, out_u.T, factor[0, :wide], factor[1, :wide], norm.reshape(-1).astype(BF16)
+    )(out_g, out_u, factor, norm)
+    return out_g.T, out_u.T, factor_g, factor_u, norm.reshape(-1)
 
 
 def solution(mesh):

time: 136 us -> 132 us (0.971)
    pallas_call x1, Pallas kernels: 126 us -> 123 us  [shards(): pl.pallas_call(functools.partial(kernel, layers, rows_total), out_shape=(...]
where the time goes in v3:
time: 132 us
  Pallas kernels  132 us (100%)
    pallas_call x1, Pallas kernels, shards(): pl.pallas_call(functools.partial(kernel, layers, rows_total), out_shape=(...  123 us
    pallas_call x1, Pallas kernels, shards(): pl.pallas_call(put, out_shape=(jax.ShapeDtypeStruct((wide, rows_total), B...  8.33 us

profile of v3, /device:TPU:0, one launch (start us, length us, event | category | flops | bytes accessed | tf_op | source)
XLA Modules:
  0.0 132.1 jit_solution(5709404039424893405)
XLA Ops:
  0.6 123.2 %shard_map.119 = (bf16[1376,4096]{1,0:T(8,128)(2,1)S(1)}, bf16[1376,4096]{1,0:T(8,128)(2,1)S(1)}, f32[2,1408]{1,0:T(2,128)S(1)}, bf16[32,128]{1,0:T(8,128)(2,1)S(1)}) custom-call(bf16[1376,256]{1,0:T(8,128)(2,1)} %bitcast.9, bf16[1376,256]{1,0:T(8,128)(2,1)} %bitcast.10, bf16[64,256]{1,0:T(8,128)(2,1)} %bitcast.11, bf16[64,256]{1,0:T(8,128)(2,1)} %bitcast.12, ...), custom_call_target="tpu_custom_call" | custom-call | tf_op jit(solution)/shard_map/pallas_call | solution.py:293
  123.8 8.3 %shard_map.120 = (bf16[1376,4096]{1,0:T(8,128)(2,1)}, bf16[1376,4096]{1,0:T(8,128)(2,1)}, f32[1376]{0:T(1024)}, f32[1376]{0:T(1024)}, bf16[32,128]{1,0:T(8,128)(2,1)}) custom-call(bf16[1376,4096]{1,0:T(8,128)(2,1)S(1)} %get-tuple-element.14.g, bf16[1376,4096]{1,0:T(8,128)(2,1)S(1)} %get-tuple-element.15.u, f32[2,1408]{1,0:T(2,128)S(1)} %get-tuple-element.16.factor, ...), custom_call_target="tpu_custom_call" | custom-call | tf_op jit(solution)/shard_map/pallas_call | solution.py:339

commit v4 on v3

--- a/solution.py
+++ b/solution.py
@@ -12,10 +12,21 @@
 BF16 = jnp.bfloat16
 SIDE = 4
 DIRS = (1, -1)
+ALONG = (0, -1, 1, 2)
 
 
 def wrap(i, n):
     return lax.rem(i + n, n)
+
+
+def is_late(core, q):
+    return jnp.logical_or(core == 0, q == 3)
+
+
+def place_of(a, along, across):
+    zero = lax.axis_index("zero")
+    dx, dy = (along, across) if a == 0 else (across, along)
+    return wrap(lax.div(zero, SIDE) + dy, SIDE) * SIDE + wrap(lax.rem(zero, SIDE) + dx, SIDE)
 
 
 def kernel(
@@ -34,9 +45,7 @@
     x, y = lax.rem(zero, SIDE), lax.div(zero, SIDE)
     train, low, high, out = (train_g, train_u), (low_g, low_u), (high_g, high_u), (out_g, out_u)
 
-    def place(a, along, across):
-        dx, dy = (along, across) if a == 0 else (across, along)
-        return wrap(y + dy, SIDE) * SIDE + wrap(x + dx, SIDE)
+    place = place_of
 
     def block(a, along, across, start, size):
         first = pl.multiple_of(place(a, along, across) * width, width)
@@ -224,19 +233,26 @@
         @pl.when(other < layer)
         def _():
             to_layer(other).start()
-    ends = []
-    for q, along in enumerate((0, -1, 1, 2)):
-        for s, d in enumerate(DIRS):
+    def end(a, s, q):
+        ref = block(a, ALONG[q], -DIRS[s], s * half, half)
+        return send(ref, ref, end_s.at[a, s, q], end_r.at[a, s, q], (place(a, 0, DIRS[s]), col))
+
+    ends = [(a, s, q) for q in range(4) for s in (0, 1) for a in (0, 1)]
+    for q in range(4):
+        for s in (0, 1):
             for a in (0, 1):
                 hops[a, s, q, s].wait_recv()
-                ref = block(a, along, -d, s * half, half)
-                ends.append(go(send(ref, ref, end_s.at[a, s, q], end_r.at[a, s, q], (place(a, 0, d), col))))
-        if q == 1:
-            for other in range(layers):
-                @pl.when(other > layer)
-                def _():
-                    from_layer(other).wait_recv()
-                    to_layer(other).start()
+
+        @pl.when(jnp.logical_not(is_late(core, q)))
+        def _():
+            for key in ends:
+                if key[2] == q:
+                    end(*key).start()
+    for other in range(layers):
+        @pl.when(other > layer)
+        def _():
+            from_layer(other).wait_recv()
+            to_layer(other).start()
     for other in range(layers):
         @pl.when(other < layer)
         def _():
@@ -258,25 +274,95 @@
                 hops[a, s, q, 1 - s].wait_recv()
     for copy in sent:
         copy.wait_send()
-    for copy in ends:
-        copy.wait_recv()
-
-
-def put(g, u, factor, norm, out_g, out_u, factor_g, factor_u, norm_out, sem):
-    pieces = sem.shape[1]
-    step = g.shape[0] // pieces
-    copies = [
-        pltpu.make_async_copy(src.at[pl.ds(i * step, step), :], dst.at[pl.ds(i * step, step), :], sem.at[j, i])
-        for i in range(pieces) for j, (src, dst) in enumerate(((g, out_g), (u, out_u)))
-    ]
-    for copy in copies:
-        copy.start()
+    for q in range(4):
+        @pl.when(jnp.logical_not(is_late(core, q)))
+        def _():
+            for key in ends:
+                if key[2] == q:
+                    end(*key).wait()
+
+
+def last_relays(out_g, out_u, _, tail, send_sem, recv_sem):
+    zero, col = lax.axis_index("zero"), lax.axis_index("cols")
+    core = lax.rem(col, 2)
+    wide, width = tail.shape[2:]
+    half = wide // 2
+    barrier = pltpu.get_barrier_semaphore()
+    for a in (0, 1):
+        for d in DIRS:
+            pl.semaphore_signal(barrier, inc=1, device_id=(place_of(a, 0, d), col), device_id_type=MESH)
+    pl.semaphore_wait(barrier, 4)
+
+    def end(a, s, q):
+        d = DIRS[s]
+        first = pl.multiple_of(place_of(a, ALONG[q], -d) * width, width)
+        rows = pl.ds(s * half, half)
+        return pltpu.make_async_remote_copy(
+            src_ref=(out_g, out_u)[a].at[rows, pl.ds(first, width)],
+            dst_ref=tail.at[a, q, rows, :],
+            send_sem=send_sem.at[a, s, q],
+            recv_sem=recv_sem.at[a, s, q],
+            device_id=(place_of(a, 0, d), col),
+            device_id_type=MESH,
+        )
+
+    def each(act):
+        for q in range(4):
+            @pl.when(is_late(core, q))
+            def _():
+                for s in (0, 1):
+                    for a in (0, 1):
+                        act(end(a, s, q))
+
+    each(lambda copy: copy.start())
+    each(lambda copy: copy.wait())
+
+
+def columns(a, along, across, width):
+    return pl.ds(pl.multiple_of(place_of(a, along, across) * width, width), width)
+
+
+def put(width, g, u, factor, norm, out_g, out_u, factor_g, factor_u, norm_out, sem):
+    core = lax.rem(lax.axis_index("cols"), 2)
+
+    def copy(a, q, k):
+        across = (0, -1, 1, 2)[k]
+        here = columns(a, ALONG[q], across, width)
+        return pltpu.make_async_copy((g, u)[a].at[:, here], (out_g, out_u)[a].at[:, here], sem.at[a, q, k])
+
+    def each(act):
+        for q in range(4):
+            for a in (0, 1):
+                for k in range(3):
+                    act(copy(a, q, k))
+
+            @pl.when(jnp.logical_not(is_late(core, q)))
+            def _():
+                for a in (0, 1):
+                    act(copy(a, q, 3))
+
+    each(lambda c: c.start())
     wide = factor_g.shape[0]
     factor_g[...] = factor[0, :wide]
     factor_u[...] = factor[1, :wide]
     norm_out[...] = norm[...]
-    for copy in copies:
-        copy.wait()
+    each(lambda c: c.wait())
+
+
+def put_tail(tail, held_g, held_u, out_g, out_u, sem):
+    core = lax.rem(lax.axis_index("cols"), 2)
+    width = tail.shape[3]
+
+    def each(act):
+        for q in range(4):
+            @pl.when(is_late(core, q))
+            def _():
+                for a in (0, 1):
+                    here = columns(a, ALONG[q], 2, width)
+                    act(pltpu.make_async_copy(tail.at[a, q], (out_g, out_u)[a].at[:, here], sem.at[a, q]))
+
+    each(lambda c: c.start())
+    each(lambda c: c.wait())
 
 
 def shards(devices, cols, train_gate, low_gate, high_gate, train_up, low_up, high_up, norm_train, norm_step):
@@ -336,21 +422,41 @@
             )
         )
     )
-    out_g, out_u, factor_g, factor_u, norm = pl.pallas_call(
-        put,
+    whole = jax.ShapeDtypeStruct((wide, rows_total), BF16)
+    ready_g, ready_u, factor_g, factor_u, norm = pl.pallas_call(
+        functools.partial(put, width),
         out_shape=(
-            jax.ShapeDtypeStruct((wide, rows_total), BF16),
-            jax.ShapeDtypeStruct((wide, rows_total), BF16),
+            whole,
+            whole,
             jax.ShapeDtypeStruct((wide,), F32),
             jax.ShapeDtypeStruct((wide,), F32),
             jax.ShapeDtypeStruct((rows, 128), BF16),
         ),
         in_specs=[vmem] * 4,
         out_specs=[hbm] * 2 + [vmem] * 3,
+        scratch_shapes=[dma((2, 4, 4))],
+        compiler_params=pltpu.CompilerParams(vmem_limit_bytes=1024 * 1024),
+    )(out_g, out_u, factor, norm)
+    tail = pl.pallas_call(
+        last_relays,
+        out_shape=pltpu.VMEM((2, 4, wide, width), BF16),
+        in_specs=[vmem] * 2 + [hbm],
+        out_specs=vmem,
+        scratch_shapes=[dma((2, 2, 4)), dma((2, 2, 4))],
+        compiler_params=pltpu.CompilerParams(
+            collective_id=1, has_side_effects=True, vmem_limit_bytes=1024 * 1024
+        ),
+    )(out_g, out_u, pltpu.with_memory_space_constraint(norm, pltpu.HBM))
+    ready_g, ready_u = pl.pallas_call(
+        put_tail,
+        out_shape=(whole, whole),
+        in_specs=[vmem, hbm, hbm],
+        out_specs=[hbm] * 2,
+        input_output_aliases={1: 0, 2: 1},
         scratch_shapes=[dma((2, 4))],
         compiler_params=pltpu.CompilerParams(vmem_limit_bytes=1024 * 1024),
-    )(out_g, out_u, factor, norm)
-    return out_g.T, out_u.T, factor_g, factor_u, norm.reshape(-1)
+    )(tail, ready_g, ready_u)
+    return ready_g.T, ready_u.T, factor_g, factor_u, norm.reshape(-1)
 
 
 def solution(mesh):

time: 132 us -> 130 us (0.985)
  Pallas kernels: 132 us -> 129 us
    pallas_call x1, Pallas kernels: 123 us -> 94.8 us  [shards(): pl.pallas_call(functools.partial(kernel, layers, rows_total), out_shape=(...]
    pallas_call x1 -> x3, Pallas kernels: 8.33 us -> 34.3 us  [the longest x1 25 us: shards(): pl.pallas_call(last_relays, out_shape=pltpu.VMEM((2, 4, wide, width), BF1...]
where the time goes in v4:
time: 130 us
  Pallas kernels  129 us (99%)
    pallas_call x1, Pallas kernels, shards(): pl.pallas_call(functools.partial(kernel, layers, rows_total), out_shape=(...  94.8 us
    pallas_call x1, Pallas kernels, shards(): pl.pallas_call(last_relays, out_shape=pltpu.VMEM((2, 4, wide, width), BF1...  25 us
    pallas_call x1, Pallas kernels, shards(): pl.pallas_call(functools.partial(put, width), out_shape=(whole, whole, ja...  6.76 us

profile of v4, /device:TPU:0, one launch (start us, length us, event | category | flops | bytes accessed | tf_op | source)
XLA Modules:
  0.0 129.7 jit_solution(10351174107533898608)
XLA Ops:
  0.6 94.8 %shard_map.119 = (bf16[1376,4096]{1,0:T(8,128)(2,1)S(1)}, bf16[1376,4096]{1,0:T(8,128)(2,1)S(1)}, f32[2,1408]{1,0:T(2,128)S(1)}, bf16[32,128]{1,0:T(8,128)(2,1)S(1)}) custom-call(bf16[1376,256]{1,0:T(8,128)(2,1)} %bitcast.11, bf16[1376,256]{1,0:T(8,128)(2,1)} %bitcast.12, bf16[64,256]{1,0:T(8,128)(2,1)} %bitcast.13, bf16[64,256]{1,0:T(8,128)(2,1)} %bitcast.14, ...), custom_call_target="tpu_custom_call" | custom-call | tf_op jit(solution)/shard_map/pallas_call | solution.py:379
  95.4 6.8 %shard_map.120 = (bf16[1376,4096]{1,0:T(8,128)(2,1)}, bf16[1376,4096]{1,0:T(8,128)(2,1)}, f32[1376]{0:T(1024)}, f32[1376]{0:T(1024)}, bf16[32,128]{1,0:T(8,128)(2,1)}) custom-call(bf16[1376,4096]{1,0:T(8,128)(2,1)S(1)} %get-tuple-element.16.g.out_g, bf16[1376,4096]{1,0:T(8,128)(2,1)S(1)} %get-tuple-element.17.u.out_u, ...), custom_call_target="tpu_custom_call" | custom-call | tf_op jit(solution)/shard_map/pallas_call | solution.py:426
  102.2 25.0 %shard_map.121.tail = bf16[2,4,1376,256]{3,2,1,0:T(8,128)(2,1)S(1)} custom-call(bf16[1376,4096]{1,0:T(8,128)(2,1)S(1)} %get-tuple-element.16.g.out_g, bf16[1376,4096]{1,0:T(8,128)(2,1)S(1)} %get-tuple-element.17.u.out_u, bf16[32,128]{1,0:T(8,128)(2,1)} %get-tuple-element.20._), custom_call_target="tpu_custom_call" | custom-call | tf_op jit(solution)/shard_map/pallas_call | solution.py:440
  127.2 2.6 %shard_map.122 = (bf16[1376,4096]{1,0:T(8,128)(2,1)}, bf16[1376,4096]{1,0:T(8,128)(2,1)}) custom-call(bf16[2,4,1376,256]{3,2,1,0:T(8,128)(2,1)S(1)} %shard_map.121.tail, bf16[1376,4096]{1,0:T(8,128)(2,1)} %get-tuple-element.21.held_g, bf16[1376,4096]{1,0:T(8,128)(2,1)} %get-tuple-element.22.held_u), custom_call_target="tpu_custom_call", output_to_operand_aliasing={{0}: (1, {}), {1}: (2, {})} | custom-call | tf_op jit(solution)/shard_map/pallas_call | solution.py:450

commit v5 on v4

--- a/solution.py
+++ b/solution.py
@@ -20,7 +20,7 @@
 
 
 def is_late(core, q):
-    return jnp.logical_or(core == 0, q == 3)
+    return jnp.logical_or(core == 1, q >= 2)
 
 
 def place_of(a, along, across):

time: 130 us -> 129 us (level)
    pallas_call x1, Pallas kernels: 25 us -> 18.4 us  [shards(): pl.pallas_call(last_relays, out_shape=pltpu.VMEM((2, 4, wide, width), BF1...]
    pallas_call x1, Pallas kernels: 94.8 us -> 101 us  [shards(): pl.pallas_call(functools.partial(kernel, layers, rows_total), out_shape=(...]
where the time goes in v5:
time: 129 us
  Pallas kernels  128 us (99%)
    pallas_call x1, Pallas kernels, shards(): pl.pallas_call(functools.partial(kernel, layers, rows_total), out_shape=(...  101 us
    pallas_call x1, Pallas kernels, shards(): pl.pallas_call(last_relays, out_shape=pltpu.VMEM((2, 4, wide, width), BF1...  18.4 us
    pallas_call x1, Pallas kernels, shards(): pl.pallas_call(functools.partial(put, width), out_shape=(whole, whole, ja...  7.6 us

profile of v5, /device:TPU:0, one launch (start us, length us, event | category | flops | bytes accessed | tf_op | source)
XLA Modules:
  0.0 128.9 jit_solution(8041842775958156799)
XLA Ops:
  0.6 100.5 %shard_map.119 = (bf16[1376,4096]{1,0:T(8,128)(2,1)S(1)}, bf16[1376,4096]{1,0:T(8,128)(2,1)S(1)}, f32[2,1408]{1,0:T(2,128)S(1)}, bf16[32,128]{1,0:T(8,128)(2,1)S(1)}) custom-call(bf16[1376,256]{1,0:T(8,128)(2,1)} %bitcast.11, bf16[1376,256]{1,0:T(8,128)(2,1)} %bitcast.12, bf16[64,256]{1,0:T(8,128)(2,1)} %bitcast.13, bf16[64,256]{1,0:T(8,128)(2,1)} %bitcast.14, ...), custom_call_target="tpu_custom_call" | custom-call | tf_op jit(solution)/shard_map/pallas_call | solution.py:379
  101.2 7.6 %shard_map.120 = (bf16[1376,4096]{1,0:T(8,128)(2,1)}, bf16[1376,4096]{1,0:T(8,128)(2,1)}, f32[1376]{0:T(1024)}, f32[1376]{0:T(1024)}, bf16[32,128]{1,0:T(8,128)(2,1)}) custom-call(bf16[1376,4096]{1,0:T(8,128)(2,1)S(1)} %get-tuple-element.16.g.out_g, bf16[1376,4096]{1,0:T(8,128)(2,1)S(1)} %get-tuple-element.17.u.out_u, ...), custom_call_target="tpu_custom_call" | custom-call | tf_op jit(solution)/shard_map/pallas_call | solution.py:426
  108.8 18.4 %shard_map.121.tail = bf16[2,4,1376,256]{3,2,1,0:T(8,128)(2,1)S(1)} custom-call(bf16[1376,4096]{1,0:T(8,128)(2,1)S(1)} %get-tuple-element.16.g.out_g, bf16[1376,4096]{1,0:T(8,128)(2,1)S(1)} %get-tuple-element.17.u.out_u, bf16[32,128]{1,0:T(8,128)(2,1)} %get-tuple-element.20._), custom_call_target="tpu_custom_call" | custom-call | tf_op jit(solution)/shard_map/pallas_call | solution.py:440
  127.2 1.7 %shard_map.122 = (bf16[1376,4096]{1,0:T(8,128)(2,1)}, bf16[1376,4096]{1,0:T(8,128)(2,1)}) custom-call(bf16[2,4,1376,256]{3,2,1,0:T(8,128)(2,1)S(1)} %shard_map.121.tail, bf16[1376,4096]{1,0:T(8,128)(2,1)} %get-tuple-element.21.held_g, bf16[1376,4096]{1,0:T(8,128)(2,1)} %get-tuple-element.22.held_u), custom_call_target="tpu_custom_call", output_to_operand_aliasing={{0}: (1, {}), {1}: (2, {})} | custom-call | tf_op jit(solution)/shard_map/pallas_call | solution.py:450

commit v6 on v5

--- a/solution.py
+++ b/solution.py
@@ -20,7 +20,7 @@
 
 
 def is_late(core, q):
-    return jnp.logical_or(core == 1, q >= 2)
+    return jnp.logical_or(core == 1, q == 3)
 
 
 def place_of(a, along, across):

time: 129 us -> 125 us (0.969)
  Pallas kernels: 128 us -> 124 us
    pallas_call x1, Pallas kernels: 18.4 us -> 10.5 us  [shards(): pl.pallas_call(last_relays, out_shape=pltpu.VMEM((2, 4, wide, width), BF1...]
    pallas_call x1, Pallas kernels: 101 us -> 104 us  [shards(): pl.pallas_call(functools.partial(kernel, layers, rows_total), out_shape=(...]
where the time goes in v6:
time: 125 us
  Pallas kernels  124 us (99%)
    pallas_call x1, Pallas kernels, shards(): pl.pallas_call(functools.partial(kernel, layers, rows_total), out_shape=(...  104 us
    pallas_call x1, Pallas kernels, shards(): pl.pallas_call(last_relays, out_shape=pltpu.VMEM((2, 4, wide, width), BF1...  10.5 us
    pallas_call x1, Pallas kernels, shards(): pl.pallas_call(functools.partial(put, width), out_shape=(whole, whole, ja...  8.03 us

profile of v6, /device:TPU:0, one launch (start us, length us, event | category | flops | bytes accessed | tf_op | source)
XLA Modules:
  0.0 124.7 jit_solution(9728661023079931917)
XLA Ops:
  0.6 104.3 %shard_map.119 = (bf16[1376,4096]{1,0:T(8,128)(2,1)S(1)}, bf16[1376,4096]{1,0:T(8,128)(2,1)S(1)}, f32[2,1408]{1,0:T(2,128)S(1)}, bf16[32,128]{1,0:T(8,128)(2,1)S(1)}) custom-call(bf16[1376,256]{1,0:T(8,128)(2,1)} %bitcast.11, bf16[1376,256]{1,0:T(8,128)(2,1)} %bitcast.12, bf16[64,256]{1,0:T(8,128)(2,1)} %bitcast.13, bf16[64,256]{1,0:T(8,128)(2,1)} %bitcast.14, ...), custom_call_target="tpu_custom_call" | custom-call | tf_op jit(solution)/shard_map/pallas_call | solution.py:379
  104.9 8.0 %shard_map.120 = (bf16[1376,4096]{1,0:T(8,128)(2,1)}, bf16[1376,4096]{1,0:T(8,128)(2,1)}, f32[1376]{0:T(1024)}, f32[1376]{0:T(1024)}, bf16[32,128]{1,0:T(8,128)(2,1)}) custom-call(bf16[1376,4096]{1,0:T(8,128)(2,1)S(1)} %get-tuple-element.16.g.out_g, bf16[1376,4096]{1,0:T(8,128)(2,1)S(1)} %get-tuple-element.17.u.out_u, ...), custom_call_target="tpu_custom_call" | custom-call | tf_op jit(solution)/shard_map/pallas_call | solution.py:426
  113.0 10.5 %shard_map.121.tail = bf16[2,4,1376,256]{3,2,1,0:T(8,128)(2,1)S(1)} custom-call(bf16[1376,4096]{1,0:T(8,128)(2,1)S(1)} %get-tuple-element.16.g.out_g, bf16[1376,4096]{1,0:T(8,128)(2,1)S(1)} %get-tuple-element.17.u.out_u, bf16[32,128]{1,0:T(8,128)(2,1)} %get-tuple-element.20._), custom_call_target="tpu_custom_call" | custom-call | tf_op jit(solution)/shard_map/pallas_call | solution.py:440
  123.5 1.2 shard_map.122

commit v7 on v6

--- a/solution.py
+++ b/solution.py
@@ -47,9 +47,8 @@
 
     place = place_of
 
-    def block(a, along, across, start, size):
-        first = pl.multiple_of(place(a, along, across) * width, width)
-        return out[a].at[pl.ds(start, size), pl.ds(first, width)]
+    def block(a, q, k, start, size, count=1):
+        return out[a].at[pl.ds(start, size), pl.ds((k * SIDE + q) * width, count * width)]
 
     def send(src, dst, ssem, rsem, to):
         return pltpu.make_async_remote_copy(
@@ -174,7 +173,7 @@
         factor_here = inverse[a, r, :]
         return (value * jnp.concatenate([factor_here, factor_here], axis=1)).astype(BF16)
 
-    def finish(a, along, source, low_ref, h):
+    def finish(a, q, source, low_ref, h):
         r = slice(h * half, (h + 1) * half)
         if source is None:
             value = latest[a, r, :]
@@ -182,42 +181,41 @@
             value = source[r, :].astype(F32) + lax.dot_general(
                 highs[a, :, r], low_ref[...], (((0,), (0,)), ((), ())), preferred_element_type=F32
             )
-        first = pl.multiple_of(place(a, along, 0) * width, width)
-        out[a][r, pl.ds(first, width)] = scaled(a, value, r)
+        out[a][r, q * width : (q + 1) * width] = scaled(a, value, r)
 
     hops = {}
 
-    def hop(a, q, along, h):
+    def hop(a, g):
+        q, count = ((0, 1), (1, 2), (3, 1))[g]
         for s, d in enumerate(DIRS):
-            ref = block(a, along, 0, h * half, half)
-            hops[a, s, q, h] = go(
-                send(ref, ref, hop_s.at[a, s, q, h], hop_r.at[a, s, q, h], (place(a, 0, d), col))
+            hops[a, s, g] = go(
+                send(block(a, q, 0, 0, wide, count), block(a, q, 1 + s, 0, wide, count),
+                     hop_s.at[a, s, g], hop_r.at[a, s, g], (place(a, 0, d), col))
             )
 
-    for h in (0, 1):
-        for a in (0, 1):
+    for a in (0, 1):
+        for h in (0, 1):
             finish(a, 0, None, None, h)
-            hop(a, 0, 0, h)
+        hop(a, 0)
 
     for copy in raws:
         copy.wait_recv()
-    far = {}
+    far = []
     for s, d in enumerate(DIRS):
         for a in (0, 1):
-            finish(a, -d, raw.at[a, s], raw_low.at[a, s], s)
-            ref = block(a, -d, 0, s * half, half)
-            far[a, s] = go(send(ref, ref, far_s.at[a, s], far_r.at[a, s], (place(a, d, 0), col)))
-    for s, d in enumerate(DIRS):
-        for a in (0, 1):
-            finish(a, -d, raw.at[a, s], raw_low.at[a, s], 1 - s)
-    for s, d in enumerate(DIRS):
-        for h in (0, 1):
-            for a in (0, 1):
-                hop(a, 1 + s, -d, h)
-    for h in (0, 1):
-        for a in (0, 1):
-            far[a, h].wait_recv()
-            hop(a, 3, 2, h)
+            finish(a, 1 + s, raw.at[a, s], raw_low.at[a, s], s)
+            far.append(go(
+                send(block(a, 1 + s, 0, s * half, half), block(a, 3, 0, s * half, half),
+                     far_s.at[a, s], far_r.at[a, s], (place(a, d, 0), col))
+            ))
+    for a in (0, 1):
+        for s in (0, 1):
+            finish(a, 1 + s, raw.at[a, s], raw_low.at[a, s], 1 - s)
+        hop(a, 1)
+    for copy in far:
+        copy.wait_recv()
+    for a in (0, 1):
+        hop(a, 2)
     for copy in norm_y:
         copy.wait_recv()
     for i in range(stack.shape[1]):
@@ -233,21 +231,21 @@
         @pl.when(other < layer)
         def _():
             to_layer(other).start()
-    def end(a, s, q):
-        ref = block(a, ALONG[q], -DIRS[s], s * half, half)
-        return send(ref, ref, end_s.at[a, s, q], end_r.at[a, s, q], (place(a, 0, DIRS[s]), col))
-
-    ends = [(a, s, q) for q in range(4) for s in (0, 1) for a in (0, 1)]
-    for q in range(4):
+    ends = [
+        send(block(a, 0, 1 + s, s * half, half, 3), block(a, 0, 3, s * half, half, 3),
+             end_s.at[a, s], end_r.at[a, s], (place(a, 0, d), col))
+        for s, d in enumerate(DIRS) for a in (0, 1)
+    ]
+    for g in range(2):
         for s in (0, 1):
             for a in (0, 1):
-                hops[a, s, q, s].wait_recv()
-
-        @pl.when(jnp.logical_not(is_late(core, q)))
-        def _():
-            for key in ends:
-                if key[2] == q:
-                    end(*key).start()
+                hops[a, s, g].wait_recv()
+
+    @pl.when(core == 0)
+    def _():
+        for copy in ends:
+            copy.start()
+
     for other in range(layers):
         @pl.when(other > layer)
         def _():
@@ -268,24 +266,22 @@
         for i in range(total.shape[0]):
             rows[parts * i + hi : parts * i + hi + 1, :] = total[i : i + 1, :]
     norm_out[...] = rows[...].astype(BF16)
-    for q in range(4):
-        for s in (0, 1):
-            for a in (0, 1):
-                hops[a, s, q, 1 - s].wait_recv()
+    for s in (0, 1):
+        for a in (0, 1):
+            hops[a, s, 2].wait_recv()
     for copy in sent:
         copy.wait_send()
-    for q in range(4):
-        @pl.when(jnp.logical_not(is_late(core, q)))
-        def _():
-            for key in ends:
-                if key[2] == q:
-                    end(*key).wait()
+
+    @pl.when(core == 0)
+    def _():
+        for copy in ends:
+            copy.wait()
 
 
 def last_relays(out_g, out_u, _, tail, send_sem, recv_sem):
     zero, col = lax.axis_index("zero"), lax.axis_index("cols")
     core = lax.rem(col, 2)
-    wide, width = tail.shape[2:]
+    wide, width = tail.shape[1], tail.shape[2] // SIDE
     half = wide // 2
     barrier = pltpu.get_barrier_semaphore()
     for a in (0, 1):
@@ -293,29 +289,30 @@
             pl.semaphore_signal(barrier, inc=1, device_id=(place_of(a, 0, d), col), device_id_type=MESH)
     pl.semaphore_wait(barrier, 4)
 
-    def end(a, s, q):
-        d = DIRS[s]
-        first = pl.multiple_of(place_of(a, ALONG[q], -d) * width, width)
-        rows = pl.ds(s * half, half)
-        return pltpu.make_async_remote_copy(
-            src_ref=(out_g, out_u)[a].at[rows, pl.ds(first, width)],
-            dst_ref=tail.at[a, q, rows, :],
-            send_sem=send_sem.at[a, s, q],
-            recv_sem=recv_sem.at[a, s, q],
-            device_id=(place_of(a, 0, d), col),
-            device_id_type=MESH,
-        )
-
-    def each(act):
-        for q in range(4):
-            @pl.when(is_late(core, q))
-            def _():
-                for s in (0, 1):
-                    for a in (0, 1):
-                        act(end(a, s, q))
-
-    each(lambda copy: copy.start())
-    each(lambda copy: copy.wait())
+    def relay(q):
+        copies = [
+            pltpu.make_async_remote_copy(
+                src_ref=(out_g, out_u)[a].at[rows, pl.ds(((1 + s) * SIDE + q) * width, (SIDE - q) * width)],
+                dst_ref=tail.at[a, rows, pl.ds(q * width, (SIDE - q) * width)],
+                send_sem=send_sem.at[a, s],
+                recv_sem=recv_sem.at[a, s],
+                device_id=(place_of(a, 0, d), col),
+                device_id_type=MESH,
+            )
+            for s, d in enumerate(DIRS) for a in (0, 1) for rows in (pl.ds(s * half, half),)
+        ]
+        for copy in copies:
+            copy.start()
+        for copy in copies:
+            copy.wait()
+
+    @pl.when(core == 0)
+    def _():
+        relay(3)
+
+    @pl.when(core == 1)
+    def _():
+        relay(0)
 
 
 def columns(a, along, across, width):
@@ -326,9 +323,9 @@
     core = lax.rem(lax.axis_index("cols"), 2)
 
     def copy(a, q, k):
-        across = (0, -1, 1, 2)[k]
-        here = columns(a, ALONG[q], across, width)
-        return pltpu.make_async_copy((g, u)[a].at[:, here], (out_g, out_u)[a].at[:, here], sem.at[a, q, k])
+        held = pl.ds((k * SIDE + q) * width, width)
+        here = columns(a, ALONG[q], ALONG[k], width)
+        return pltpu.make_async_copy((g, u)[a].at[:, held], (out_g, out_u)[a].at[:, here], sem.at[a, q, k])
 
     def each(act):
         for q in range(4):
@@ -351,7 +348,7 @@
 
 def put_tail(tail, held_g, held_u, out_g, out_u, sem):
     core = lax.rem(lax.axis_index("cols"), 2)
-    width = tail.shape[3]
+    width = tail.shape[2] // SIDE
 
     def each(act):
         for q in range(4):
@@ -359,7 +356,7 @@
             def _():
                 for a in (0, 1):
                     here = columns(a, ALONG[q], 2, width)
-                    act(pltpu.make_async_copy(tail.at[a, q], (out_g, out_u)[a].at[:, here], sem.at[a, q]))
+                    act(pltpu.make_async_copy(tail.at[a, :, pl.ds(q * width, width)], (out_g, out_u)[a].at[:, here], sem.at[a, q]))
 
     each(lambda c: c.start())
     each(lambda c: c.wait())
@@ -405,8 +402,8 @@
             dma((2, 2, 4)), dma((2, 2, 4)),
             dma((2, 2)), dma((2, 2)),
             dma((2, 2)), dma((2, 2)),
-            dma((2, 2, 4, 2)), dma((2, 2, 4, 2)),
-            dma((2, 2, 4)), dma((2, 2, 4)),
+            dma((2, 2, 3)), dma((2, 2, 3)),
+            dma((2, 2)), dma((2, 2)),
             dma((5, 3)), dma((5, 3)),
             dma((layers,)), dma((layers,)),
         ],
@@ -439,10 +436,10 @@
     )(out_g, out_u, factor, norm)
     tail = pl.pallas_call(
         last_relays,
-        out_shape=pltpu.VMEM((2, 4, wide, width), BF16),
+        out_shape=pltpu.VMEM((2, wide, SIDE * width), BF16),
         in_specs=[vmem] * 2 + [hbm],
         out_specs=vmem,
-        scratch_shapes=[dma((2, 2, 4)), dma((2, 2, 4))],
+        scratch_shapes=[dma((2, 2)), dma((2, 2))],
         compiler_params=pltpu.CompilerParams(
             collective_id=1, has_side_effects=True, vmem_limit_bytes=1024 * 1024
         ),

time: 125 us -> 123 us (0.984)
  no operation moved by 1% of the time
where the time goes in v7:
time: 123 us
  Pallas kernels  123 us (100%)
    pallas_call x1, Pallas kernels, shards(): pl.pallas_call(functools.partial(kernel, layers, rows_total), out_shape=(...  104 us
    pallas_call x1, Pallas kernels, shards(): pl.pallas_call(last_relays, out_shape=pltpu.VMEM((2, wide, SIDE * width),...  9.32 us
    pallas_call x1, Pallas kernels, shards(): pl.pallas_call(functools.partial(put, width), out_shape=(whole, whole, ja...  8.02 us

profile of v7, /device:TPU:0, one launch (start us, length us, event | category | flops | bytes accessed | tf_op | source)
XLA Modules:
  0.0 123.4 jit_solution(14442457570813609712)
XLA Ops:
  0.6 104.2 %shard_map.119 = (bf16[1376,4096]{1,0:T(8,128)(2,1)S(1)}, bf16[1376,4096]{1,0:T(8,128)(2,1)S(1)}, f32[2,1408]{1,0:T(2,128)S(1)}, bf16[32,128]{1,0:T(8,128)(2,1)S(1)}) custom-call(bf16[1376,256]{1,0:T(8,128)(2,1)} %bitcast.11, bf16[1376,256]{1,0:T(8,128)(2,1)} %bitcast.12, bf16[64,256]{1,0:T(8,128)(2,1)} %bitcast.13, bf16[64,256]{1,0:T(8,128)(2,1)} %bitcast.14, ...), custom_call_target="tpu_custom_call" | custom-call | tf_op jit(solution)/shard_map/pallas_call | solution.py:376
  104.8 8.0 %shard_map.120 = (bf16[1376,4096]{1,0:T(8,128)(2,1)}, bf16[1376,4096]{1,0:T(8,128)(2,1)}, f32[1376]{0:T(1024)}, f32[1376]{0:T(1024)}, bf16[32,128]{1,0:T(8,128)(2,1)}) custom-call(bf16[1376,4096]{1,0:T(8,128)(2,1)S(1)} %get-tuple-element.16.g.out_g, bf16[1376,4096]{1,0:T(8,128)(2,1)S(1)} %get-tuple-element.17.u.out_u, ...), custom_call_target="tpu_custom_call" | custom-call | tf_op jit(solution)/shard_map/pallas_call | solution.py:423
  112.9 9.3 %shard_map.121.tail = bf16[2,1376,1024]{2,1,0:T(8,128)(2,1)S(1)} custom-call(bf16[1376,4096]{1,0:T(8,128)(2,1)S(1)} %get-tuple-element.16.g.out_g, bf16[1376,4096]{1,0:T(8,128)(2,1)S(1)} %get-tuple-element.17.u.out_u, bf16[32,128]{1,0:T(8,128)(2,1)} %get-tuple-element.20._), custom_call_target="tpu_custom_call" | custom-call | tf_op jit(solution)/shard_map/pallas_call | solution.py:437
  122.2 1.2 shard_map.122

commit v8 on v7

--- a/solution.py
+++ b/solution.py
@@ -39,8 +39,8 @@
 ):
     wide, width = own.shape[1:]
     half = wide // 2
-    cut = half // 2 // 16 * 16
-    pieces = ((0, cut), (cut, half - cut), (half, cut), (half + cut, half - cut))
+    cuts = [0] + [wide * part // 16 // 16 * 16 for part in (6, 10, 13)] + [wide]
+    pieces = [(lo, hi - lo) for lo, hi in zip(cuts, cuts[1:])]
     zero, col = lax.axis_index("zero"), lax.axis_index("cols")
     x, y = lax.rem(zero, SIDE), lax.div(zero, SIDE)
     train, low, high, out = (train_g, train_u), (low_g, low_u), (high_g, high_u), (out_g, out_u)
@@ -80,6 +80,28 @@
     for load in loads:
         load.start()
 
+    pl.semaphore_wait(barrier, len(x_peers) + len(y_peers) + len(c_peers) + layer)
+
+    sent = []
+
+    def go(copy):
+        copy.start()
+        sent.append(copy)
+        return copy
+
+    def send_raw(p):
+        start, size = pieces[p]
+        return [
+            go(send(train[a].at[pl.ds(start, size), :], raw.at[a, s, pl.ds(start, size), :],
+                    raw_s.at[a, s, p], raw_r.at[a, s, p], (place(a, d, 0), col)))
+            for a in (0, 1) for s, d in enumerate(DIRS)
+        ]
+
+    raws = send_raw(0)
+    raws += [
+        go(send(low[a], raw_low.at[a, s], low_s.at[a, s], low_r.at[a, s], (place(a, d, 0), col)))
+        for a in (0, 1) for s, d in enumerate(DIRS)
+    ]
     for load in gain_loads:
         load.wait()
     value = gains[0] + gains[1]
@@ -87,28 +109,6 @@
     group = lax.broadcasted_iota(jnp.int32, (1, 128), 1) // value.shape[1]
     mine = lax.rem(col, 128 // value.shape[1])
     norm[core, zero] = jnp.where(group == mine, spread, jnp.zeros_like(spread))
-    pl.semaphore_wait(barrier, len(x_peers) + len(y_peers) + len(c_peers) + layer)
-
-    sent = []
-
-    def go(copy):
-        copy.start()
-        sent.append(copy)
-        return copy
-
-    def send_raw(p):
-        start, size = pieces[p]
-        return [
-            go(send(train[a].at[pl.ds(start, size), :], raw.at[a, s, pl.ds(start, size), :],
-                    raw_s.at[a, s, p], raw_r.at[a, s, p], (place(a, d, 0), col)))
-            for a in (0, 1) for s, d in enumerate(DIRS)
-        ]
-
-    raws = send_raw(0)
-    raws += [
-        go(send(low[a], raw_low.at[a, s], low_s.at[a, s], low_r.at[a, s], (place(a, d, 0), col)))
-        for a in (0, 1) for s, d in enumerate(DIRS)
-    ]
     norm_c = [
         go(send(norm.at[core, zero], norm.at[core, zero], small_s.at[0, i], small_r.at[0, i], peer))
         for i, peer in enumerate(c_peers)

time: 123 us -> 123 us (level)
  no operation moved by 1% of the time
where the time goes in v8:
time: 123 us
  Pallas kernels  123 us (100%)
    pallas_call x1, Pallas kernels, shards(): pl.pallas_call(functools.partial(kernel, layers, rows_total), out_shape=(...  104 us
    pallas_call x1, Pallas kernels, shards(): pl.pallas_call(last_relays, out_shape=pltpu.VMEM((2, wide, SIDE * width),...  9.32 us
    pallas_call x1, Pallas kernels, shards(): pl.pallas_call(functools.partial(put, width), out_shape=(whole, whole, ja...  8.02 us

profile of v8, /device:TPU:0, one launch (start us, length us, event | category | flops | bytes accessed | tf_op | source)
XLA Modules:
  0.0 123.4 jit_solution(11288266219505666978)
XLA Ops:
  0.6 104.2 %shard_map.119 = (bf16[1376,4096]{1,0:T(8,128)(2,1)S(1)}, bf16[1376,4096]{1,0:T(8,128)(2,1)S(1)}, f32[2,1408]{1,0:T(2,128)S(1)}, bf16[32,128]{1,0:T(8,128)(2,1)S(1)}) custom-call(bf16[1376,256]{1,0:T(8,128)(2,1)} %bitcast.11, bf16[1376,256]{1,0:T(8,128)(2,1)} %bitcast.12, bf16[64,256]{1,0:T(8,128)(2,1)} %bitcast.13, bf16[64,256]{1,0:T(8,128)(2,1)} %bitcast.14, ...), custom_call_target="tpu_custom_call" | custom-call | tf_op jit(solution)/shard_map/pallas_call | solution.py:376
  104.8 8.0 %shard_map.120 = (bf16[1376,4096]{1,0:T(8,128)(2,1)}, bf16[1376,4096]{1,0:T(8,128)(2,1)}, f32[1376]{0:T(1024)}, f32[1376]{0:T(1024)}, bf16[32,128]{1,0:T(8,128)(2,1)}) custom-call(bf16[1376,4096]{1,0:T(8,128)(2,1)S(1)} %get-tuple-element.16.g.out_g, bf16[1376,4096]{1,0:T(8,128)(2,1)S(1)} %get-tuple-element.17.u.out_u, ...), custom_call_target="tpu_custom_call" | custom-call | tf_op jit(solution)/shard_map/pallas_call | solution.py:423
  112.9 9.3 %shard_map.121.tail = bf16[2,1376,1024]{2,1,0:T(8,128)(2,1)S(1)} custom-call(bf16[1376,4096]{1,0:T(8,128)(2,1)S(1)} %get-tuple-element.16.g.out_g, bf16[1376,4096]{1,0:T(8,128)(2,1)S(1)} %get-tuple-element.17.u.out_u, bf16[32,128]{1,0:T(8,128)(2,1)} %get-tuple-element.20._), custom_call_target="tpu_custom_call" | custom-call | tf_op jit(solution)/shard_map/pallas_call | solution.py:437
  122.2 1.2 shard_map.122
